TPU v7x, 32 devices: a whole 2x2x4 slice. The times are simulated.
32 devices in a mesh: qa: 16 (over z, x, core), qb: 2 (over y).
Axes of the slice: x: 2, y: 2, z: 4, core: 2. Of those that a mesh axis runs over, the one named last changes fastest.
Arguments:
- wave_parts: float32 [2, 256, 128, 128], P(None, ('qa', 'qb')), may hold values from -6 to 6
- level_table: float32 [256, 128, 128], P(('qa', 'qb')), may hold values from -2 to 2
- phase_angles: float32 [2, 128], replicated, may hold values from 0.3 to 1.2
Outputs:
- final_parts: float32 [2, 256, 128, 128], P(None, ('qa', 'qb'))
All inputs are finite; a program needn't handle non-finite values.
Results may differ from a plain program's by a relative error of at most 0.0003.
Values sent between devices are 32-bit elements; how exact they have to be, the bound alone decides.
A program may use at most 64 MiB of HBM per device.

v0:
```python
import functools

import jax
import jax.numpy as jnp
import numpy as np
from jax import lax
from jax.experimental import pallas as pl
from jax.experimental.pallas import tpu as pltpu
from jax.sharding import PartitionSpec as P

MESH = pl.DeviceIdType.MESH
TURN_MOST = 2.5


def fit_even(function, degree):
    top = TURN_MOST**2
    nodes = (np.cos(np.pi * (np.arange(64) + 0.5) / 64) + 1) * top / 2
    fit = np.polynomial.chebyshev.Chebyshev.fit(nodes, function(np.sqrt(nodes)), degree, domain=[0, top])
    return [float(c) for c in fit.convert(kind=np.polynomial.Polynomial).coef]


COS = fit_even(np.cos, 6)
SIN = fit_even(lambda t: np.sin(t) / t, 5)


def horner(coefs, u, scale):
    total = jnp.float32(coefs[-1] * scale)
    for c in coefs[-2::-1]:
        total = total * u + jnp.float32(c * scale)
    return total


def cos_sin(turn, scale):
    u = turn * turn
    return horner(COS, u, scale), turn * horner(SIN, u, scale)


def sign_table(count):
    both = lax.broadcasted_iota(jnp.int32, (count, count), 0) & lax.broadcasted_iota(jnp.int32, (count, count), 1)
    shift = 1
    while shift < count.bit_length():
        shift *= 2
    while shift > 1:
        shift //= 2
        both = both ^ (both >> shift)
    return (1 - 2 * (both & 1)).astype(jnp.float32).astype(jnp.bfloat16)


def mix_lead(x):
    n = x.shape[0]
    half = 1
    while half < n:
        y = x.reshape((n // (2 * half), 2, half) + x.shape[1:])
        x = jnp.stack([y[:, 0] + y[:, 1], y[:, 0] - y[:, 1]], axis=1).reshape(x.shape)
        half *= 2
    return x


def dot(a, b):
    return jnp.dot(a, b, preferred_element_type=jnp.float32)


def halves(x):
    hi = x.astype(jnp.bfloat16)
    return hi, (x - hi.astype(jnp.float32)).astype(jnp.bfloat16)


def mix_rows_lanes(rows, lanes, x, y):
    hi, lo = halves(jnp.concatenate([x, y], axis=1))
    both = dot(rows, hi) + dot(rows, lo)
    width = x.shape[1]
    out = []
    for part in (both[:, :width], both[:, width:]):
        hi, lo = halves(part)
        out.append(dot(hi, lanes) + dot(lo, lanes))
    return out


def kernel(
    na, nb, scales, wave_hbm, level_hbm, angle_hbm, out_ref,
    wave, level, angle, rows_table, lanes_table, mixed, send0, got0, send1, got1, levels, cosine, sine,
    load_sem, own_sem, ssem, rsem, level_sem,
):
    n = na * nb
    cuts, _, _, step, lanes = send0.shape
    qa, qb = lax.axis_index("qa"), lax.axis_index("qb")
    me = qa * nb + qb
    group = 4

    def flips(q, count):
        found = [q]
        bit = 1
        while bit < count:
            change = bit - 2 * bit * lax.rem(q // bit, 2)
            found = found + [f + change for f in found]
            bit *= 2
        return found

    to_as, to_bs = flips(qa, na), flips(qb, nb)
    order = [(ka, kb) for ka in far_first(na) for kb in range(nb) if ka or kb]
    peers = [(to_as[ka], to_bs[kb], to_as[ka] * nb + to_bs[kb]) for ka, kb in order]

    load_wave = pltpu.make_async_copy(wave_hbm, wave, load_sem.at[0])
    load_level = pltpu.make_async_copy(level_hbm, level, load_sem.at[1])
    load_angle = pltpu.make_async_copy(angle_hbm, angle, load_sem.at[2])
    load_level.start()
    load_angle.start()
    load_wave.start()

    barrier = pltpu.get_barrier_semaphore()
    for to_a, to_b, _ in peers[::-1]:
        pl.semaphore_signal(barrier, inc=1, device_id=(to_a, to_b), device_id_type=MESH)

    load_level.wait()
    pl.semaphore_wait(barrier, n - 1)

    def exchange(source, target, own, sent, got):
        pltpu.make_async_copy(source.at[me], target.at[me], own).start()
        for to_a, to_b, to in peers:
            pltpu.make_async_remote_copy(
                src_ref=source.at[to], dst_ref=target.at[me], send_sem=sent, recv_sem=got,
                device_id=(to_a, to_b), device_id_type=MESH,
            ).start()

    def received(source, target, own, got):
        pltpu.make_async_copy(source.at[me], target.at[me], own).wait()
        rest = target.at[pl.ds(0, n - 1)]
        pltpu.make_async_copy(rest, rest, got).wait()

    def left(source, sent):
        rest = source.at[pl.ds(0, n - 1)]
        pltpu.make_async_copy(rest, rest, sent).wait()

    exchange(level, levels, level_sem.at[0], level_sem.at[1], level_sem.at[2])
    rows_table[...] = sign_table(n * step)
    lanes_table[...] = sign_table(lanes)
    load_angle.wait()
    load_wave.wait()

    first = angle[0:1, :]

    @pl.loop(0, cuts)
    def _(cut):
        held = pl.ds(pl.multiple_of(cut * step, step), step)
        c, s = cos_sin(first * level[:, held, :].reshape(n * step, lanes), scales[0])
        x = wave[0, :, held, :].reshape(n * step, lanes)
        y = wave[1, :, held, :].reshape(n * step, lanes)
        done = mix_rows_lanes(rows_table[...], lanes_table[...], x * c + y * s, y * c - x * s)
        for part in range(2):
            mixed[cut, part] = done[part].reshape(n, step, lanes)

    for part in range(2):

        @pl.loop(0, n // group)
        def _(i):
            ds = pl.ds(i * group, group)
            send0[:, ds, part] = mix_lead(mixed[:, part, ds])

    @pl.loop(0, cuts)
    def _(cut):
        exchange(send0.at[cut], got0.at[cut], own_sem.at[0, cut], ssem.at[0, cut], rsem.at[0, cut])

    received(level, levels, level_sem.at[0], level_sem.at[2])
    second = angle[1:2, :]

    @pl.loop(0, n)
    def _(d):
        c, s = cos_sin(second * levels[d], scales[1])
        cosine[d] = c
        sine[d] = s

    @pl.loop(0, cuts)
    def _(cut):
        received(send0.at[cut], got0.at[cut], own_sem.at[0, cut], rsem.at[0, cut])
        held = pl.ds(pl.multiple_of(cut * step, step), step)
        x, y = mix_lead(got0[cut, :, 0]), mix_lead(got0[cut, :, 1])
        c, s = cosine[:, held, :], sine[:, held, :]
        send1[cut, :, 0] = mix_lead(x * c + y * s)
        send1[cut, :, 1] = mix_lead(y * c - x * s)
        exchange(send1.at[cut], got1.at[cut], own_sem.at[1, cut], ssem.at[1, cut], rsem.at[1, cut])

    @pl.loop(0, cuts)
    def _(cut):
        received(send1.at[cut], got1.at[cut], own_sem.at[1, cut], rsem.at[1, cut])
        x, y = (got1[cut, :, part].reshape(n * step, lanes) for part in range(2))
        done = mix_rows_lanes(rows_table[...], lanes_table[...], x, y)
        for part in range(2):
            mixed[cut, part] = done[part].reshape(n, step, lanes)

    for part in range(2):

        @pl.loop(0, n // group)
        def _(i):
            ds = pl.ds(i * group, group)
            done = mix_lead(mixed[:, part, ds])
            for cut in range(cuts):
                out_ref[part, ds, cut * step : (cut + 1) * step, :] = done[cut]

    left(level, level_sem.at[1])

    @pl.loop(0, cuts)
    def _(cut):
        left(send0.at[cut], ssem.at[0, cut])
        left(send1.at[cut], ssem.at[1, cut])


def far_first(count):
    quarter = count // 4
    low = [*range(0, quarter, 2), *range(1, quarter, 2)]
    return [high * quarter + k for high in (2, 3, 1, 0) for k in low] if quarter else range(count - 1, -1, -1)


STEP = 16


def body(wave_parts, level_table, phase_angles):
    na, nb = lax.axis_size("qa"), lax.axis_size("qb")
    n = na * nb
    _, blocks, rows, lanes = wave_parts.shape
    piece = blocks * rows // n
    step = min(STEP, piece)
    cuts = piece // step
    bits = (n * blocks * rows * lanes).bit_length() - 1
    scales = (2.0 ** -(bits // 2), 2.0 ** -(bits - bits // 2))
    hbm = pl.BlockSpec(memory_space=pl.ANY)
    f32 = jnp.float32
    flat = (2, n, piece, lanes)
    state = pltpu.VMEM((cuts, n, 2, step, lanes), f32)
    table = pltpu.VMEM((n, piece, lanes), f32)
    result = pl.pallas_call(
        functools.partial(kernel, na, nb, scales),
        out_shape=jax.ShapeDtypeStruct(flat, f32),
        in_specs=[hbm, hbm, hbm],
        out_specs=pl.BlockSpec(memory_space=pltpu.VMEM),
        scratch_shapes=[
            pltpu.VMEM(flat, f32),
            table,
            pltpu.VMEM(phase_angles.shape, f32),
            pltpu.VMEM((n * step, n * step), jnp.bfloat16),
            pltpu.VMEM((lanes, lanes), jnp.bfloat16),
            pltpu.VMEM((cuts, 2, n, step, lanes), f32),
            state, state, state, state, table, table, table,
            pltpu.SemaphoreType.DMA((3,)),
            pltpu.SemaphoreType.DMA((2, cuts)),
            pltpu.SemaphoreType.DMA((2, cuts)),
            pltpu.SemaphoreType.DMA((2, cuts)),
            pltpu.SemaphoreType.DMA((3,)),
        ],
        compiler_params=pltpu.CompilerParams(
            collective_id=0, has_side_effects=True, vmem_limit_bytes=62 * 2**20
        ),
    )(wave_parts.reshape(flat), level_table.reshape(n, piece, lanes), phase_angles)
    return result.reshape(wave_parts.shape)


def solution(mesh):
    in_specs = (P(None, ("qa", "qb"), None, None), P(("qa", "qb"), None, None), P())
    out_specs = P(None, ("qa", "qb"), None, None)
    return jax.shard_map(body, mesh=mesh, in_specs=in_specs, out_specs=out_specs, check_vma=False)
```

profile of v0, /device:TPU:17, one launch (start us, length us, event | category | flops | bytes accessed | tf_op | source)
XLA Modules:
  0.0 66.9 jit_solution(11659983474561218905)
XLA Ops:
  0.0 64.6 %shard_map.37 = f32[2,32,32,128]{3,2,1,0:T(8,128)} custom-call(f32[2,32,32,128]{3,2,1,0:T(8,128)} %bitcast.4, f32[32,32,128]{2,1,0:T(8,128)} %bitcast.5, f32[2,128]{1,0:T(2,128)} %angle_hbm.1), custom_call_target="tpu_custom_call" | custom-call | tf_op jit(solution)/shard_map/pallas_call | solution.py:230
  64.6 2.3 %copy.5 = f32[2,8,128,128]{3,2,1,0:T(8,128)} copy(f32[2,8,128,128]{3,2,1,0:T(8,128)} %bitcast.3) | data formatting | bytes 2097152
where the time goes:
time: 67.2 us; the launch traced here: 66.9 us
  Pallas kernels  64.6 us (96%)
  local copies, waits for them, and re-layouts  2.3 us (3%)
    pallas_call x1, Pallas kernels, body(): pl.pallas_call(functools.partial(kernel, na, nb, scales), out_shape=jax.S...  64.6 us
    unnamed x1, local copies, waits for them, and re-layouts  2.3 us

commit v1 on v0

--- a/solution.py
+++ b/solution.py
@@ -54,6 +54,18 @@
         x = jnp.stack([y[:, 0] + y[:, 1], y[:, 0] - y[:, 1]], axis=1).reshape(x.shape)
         half *= 2
     return x
+
+
+def mix_list(parts):
+    half = 1
+    while half < len(parts):
+        mixed = list(parts)
+        for k in range(len(parts)):
+            if not k & half:
+                mixed[k], mixed[k + half] = parts[k] + parts[k + half], parts[k] - parts[k + half]
+        parts = mixed
+        half *= 2
+    return parts
 
 
 def dot(a, b):
@@ -175,26 +187,26 @@
         held = pl.ds(pl.multiple_of(cut * step, step), step)
         x, y = mix_lead(got0[cut, :, 0]), mix_lead(got0[cut, :, 1])
         c, s = cosine[:, held, :], sine[:, held, :]
-        send1[cut, :, 0] = mix_lead(x * c + y * s)
-        send1[cut, :, 1] = mix_lead(y * c - x * s)
-        exchange(send1.at[cut], got1.at[cut], own_sem.at[1, cut], ssem.at[1, cut], rsem.at[1, cut])
-
-    @pl.loop(0, cuts)
-    def _(cut):
-        received(send1.at[cut], got1.at[cut], own_sem.at[1, cut], rsem.at[1, cut])
-        x, y = (got1[cut, :, part].reshape(n * step, lanes) for part in range(2))
+        x, y = (x * c + y * s).reshape(n * step, lanes), (y * c - x * s).reshape(n * step, lanes)
         done = mix_rows_lanes(rows_table[...], lanes_table[...], x, y)
         for part in range(2):
-            mixed[cut, part] = done[part].reshape(n, step, lanes)
-
-    for part in range(2):
-
-        @pl.loop(0, n // group)
-        def _(i):
-            ds = pl.ds(i * group, group)
-            done = mix_lead(mixed[:, part, ds])
-            for cut in range(cuts):
-                out_ref[part, ds, cut * step : (cut + 1) * step, :] = done[cut]
+            send1[cut, :, part] = done[part].reshape(n, step, lanes)
+        exchange(send1.at[cut], got1.at[cut], own_sem.at[1, cut], ssem.at[1, cut], rsem.at[1, cut])
+
+    few = min(8, step)
+    for cut in range(cuts):
+        received(send1.at[cut], got1.at[cut], own_sem.at[1, cut], rsem.at[1, cut])
+        last = cut == cuts - 1
+
+        for part in range(2):
+            for row in range(0, step, few):
+                done = mix_lead(got1[cut, :, part, row : row + few])
+                if not last:
+                    mixed[cut, part, :, row : row + few] = done
+                    continue
+                parts = [mixed[k, part, :, row : row + few] for k in range(cut)] + [done]
+                for k, value in enumerate(mix_list(parts)):
+                    out_ref[part, :, k * step + row : k * step + row + few, :] = value
 
     left(level, level_sem.at[1])
 
@@ -202,6 +214,12 @@
     def _(cut):
         left(send0.at[cut], ssem.at[0, cut])
         left(send1.at[cut], ssem.at[1, cut])
+
+
+def put_out(state_ref, out_hbm, sem):
+    copy = pltpu.make_async_copy(state_ref, out_hbm, sem)
+    copy.start()
+    copy.wait()
 
 
 def far_first(count):
@@ -211,6 +229,7 @@
 
 
 STEP = 16
+SPACE = 40 * 2**20
 
 
 def body(wave_parts, level_table, phase_angles):
@@ -222,14 +241,14 @@
     cuts = piece // step
     bits = (n * blocks * rows * lanes).bit_length() - 1
     scales = (2.0 ** -(bits // 2), 2.0 ** -(bits - bits // 2))
-    hbm = pl.BlockSpec(memory_space=pl.ANY)
+    hbm = pl.BlockSpec(memory_space=pltpu.HBM)
     f32 = jnp.float32
     flat = (2, n, piece, lanes)
     state = pltpu.VMEM((cuts, n, 2, step, lanes), f32)
     table = pltpu.VMEM((n, piece, lanes), f32)
     result = pl.pallas_call(
         functools.partial(kernel, na, nb, scales),
-        out_shape=jax.ShapeDtypeStruct(flat, f32),
+        out_shape=pltpu.VMEM(flat, f32),
         in_specs=[hbm, hbm, hbm],
         out_specs=pl.BlockSpec(memory_space=pltpu.VMEM),
         scratch_shapes=[
@@ -247,9 +266,20 @@
             pltpu.SemaphoreType.DMA((3,)),
         ],
         compiler_params=pltpu.CompilerParams(
-            collective_id=0, has_side_effects=True, vmem_limit_bytes=62 * 2**20
+            collective_id=0, has_side_effects=True, vmem_limit_bytes=SPACE
         ),
-    )(wave_parts.reshape(flat), level_table.reshape(n, piece, lanes), phase_angles)
+    )(*(
+        pltpu.with_memory_space_constraint(x, pltpu.HBM)
+        for x in (wave_parts.reshape(flat), level_table.reshape(n, piece, lanes), phase_angles)
+    ))
+    result = pl.pallas_call(
+        put_out,
+        out_shape=jax.ShapeDtypeStruct(flat, f32),
+        in_specs=[pl.BlockSpec(memory_space=pltpu.VMEM)],
+        out_specs=hbm,
+        scratch_shapes=[pltpu.SemaphoreType.DMA],
+        compiler_params=pltpu.CompilerParams(vmem_limit_bytes=4 * 2**20),
+    )(result)
     return result.reshape(wave_parts.shape)
 
 

time: 67.2 us -> 64.1 us (0.954)
  local copies, waits for them, and re-layouts: 2.3 us -> 0 us
  Pallas kernels: 64.6 us -> 63.8 us
    unnamed x1 -> x0, local copies, waits for them, and re-layouts: 2.3 us -> none
    pallas_call x1 -> x2, Pallas kernels: 64.6 us -> 63.8 us  [the longest x1 62.8 us: body(): pl.pallas_call(functools.partial(kernel, na, nb, scales), out_shape=pltpu...]
where the time goes in v1:
time: 64.1 us; the launch traced here: 63.8 us
  Pallas kernels  63.8 us (100%)
    pallas_call x1, Pallas kernels, body(): pl.pallas_call(functools.partial(kernel, na, nb, scales), out_shape=pltpu...  62.8 us

profile of v1, /device:TPU:17, one launch (start us, length us, event | category | flops | bytes accessed | tf_op | source)
XLA Modules:
  0.0 63.8 jit_solution(17425384116672522696)
XLA Ops:
  0.0 62.8 %shard_map.37.state_ref = f32[2,32,32,128]{3,2,1,0:T(8,128)S(1)} custom-call(f32[2,32,32,128]{3,2,1,0:T(8,128)} %bitcast.3, f32[32,32,128]{2,1,0:T(8,128)} %bitcast.4, f32[2,128]{1,0:T(2,128)} %angle_hbm.1), custom_call_target="tpu_custom_call" | custom-call | tf_op jit(solution)/shard_map/pallas_call | solution.py:249
  62.8 1.0 %shard_map.38 = f32[2,32,32,128]{3,2,1,0:T(8,128)} custom-call(f32[2,32,32,128]{3,2,1,0:T(8,128)S(1)} %shard_map.37.state_ref), custom_call_target="tpu_custom_call" | custom-call | tf_op jit(solution)/shard_map/pallas_call | solution.py:275

commit v2 on v1

--- a/solution.py
+++ b/solution.py
@@ -91,7 +91,7 @@
 def kernel(
     na, nb, scales, wave_hbm, level_hbm, angle_hbm, out_ref,
     wave, level, angle, rows_table, lanes_table, mixed, send0, got0, send1, got1, levels, cosine, sine,
-    load_sem, own_sem, ssem, rsem, level_sem,
+    load_sem, own_sem, ssem, rsem, level_sem, greet_sem,
 ):
     n = na * nb
     cuts, _, _, step, lanes = send0.shape
@@ -119,13 +119,6 @@
     load_angle.start()
     load_wave.start()
 
-    barrier = pltpu.get_barrier_semaphore()
-    for to_a, to_b, _ in peers[::-1]:
-        pl.semaphore_signal(barrier, inc=1, device_id=(to_a, to_b), device_id_type=MESH)
-
-    load_level.wait()
-    pl.semaphore_wait(barrier, n - 1)
-
     def exchange(source, target, own, sent, got):
         pltpu.make_async_copy(source.at[me], target.at[me], own).start()
         for to_a, to_b, to in peers:
@@ -143,7 +136,55 @@
         rest = source.at[pl.ds(0, n - 1)]
         pltpu.make_async_copy(rest, rest, sent).wait()
 
-    exchange(level, levels, level_sem.at[0], level_sem.at[1], level_sem.at[2])
+    inner = min(na, 4)
+    depth = na // inner
+    z, low = qa // inner, lax.rem(qa, inner)
+    to_low = flips(low, inner)
+
+    def reach(hop, m, k):
+        return abs(hop) + m // 2 + k.bit_count()
+
+    offsets = [
+        (hop, m, k)
+        for hop in sorted(range(1 - depth, depth), key=lambda h: -abs(h))
+        for m in range(inner)
+        for k in range(nb)
+        if hop or m or k
+    ]
+    furthest = max(reach(*offset) for offset in offsets)
+
+    def each(chosen, act):
+        for hop, m, k in chosen:
+            there = z + hop
+            found = functools.partial(act, there * inner + to_low[m], to_bs[k])
+            if hop:
+                pl.when((there >= 0) & (there < depth))(found)
+            else:
+                found()
+
+    def greet(count, sem, chosen):
+        each(chosen, lambda a, b: pl.semaphore_signal(sem, inc=1, device_id=(a, b), device_id_type=MESH))
+        sides = jnp.where(z > 0, 1, 0) + jnp.where(z < depth - 1, 1, 0)
+        pl.semaphore_wait(sem, count(False) + sides * count(True))
+
+    def send_level(a, b):
+        pltpu.make_async_remote_copy(
+            src_ref=level.at[a * nb + b], dst_ref=levels.at[me], send_sem=level_sem.at[1], recv_sem=level_sem.at[2],
+            device_id=(a, b), device_id_type=MESH,
+        ).start()
+
+    for stage in range(furthest):
+        near = [o for o in offsets if reach(*o) <= 1 and (stage == 0 or reach(*o) == 1 and o[1] % 2 == 0)]
+
+        def count(along, near=near):
+            return sum(o[0] == 1 if along else o[0] == 0 for o in near)
+
+        greet(count, pltpu.get_barrier_semaphore() if stage == 0 else greet_sem.at[stage - 1], near)
+        if stage == 0:
+            load_level.wait()
+            pltpu.make_async_copy(level.at[me], levels.at[me], level_sem.at[0]).start()
+        each([o for o in offsets if reach(*o) == stage + 1 or stage == 0 and reach(*o) == 0], send_level)
+
     rows_table[...] = sign_table(n * step)
     lanes_table[...] = sign_table(lanes)
     load_angle.wait()
@@ -264,6 +305,7 @@
             pltpu.SemaphoreType.DMA((2, cuts)),
             pltpu.SemaphoreType.DMA((2, cuts)),
             pltpu.SemaphoreType.DMA((3,)),
+            pltpu.SemaphoreType.REGULAR((n.bit_length() + na,)),
         ],
         compiler_params=pltpu.CompilerParams(
             collective_id=0, has_side_effects=True, vmem_limit_bytes=SPACE

time: 64.1 us -> 64.2 us (level); the launches traced: 63.8 us -> 63.2 us
  no operation moved by 1% of the time
where the time goes in v2:
time: 64.2 us; the launch traced here: 63.2 us
  Pallas kernels  63.2 us (98%)
    pallas_call x1, Pallas kernels, body(): pl.pallas_call(functools.partial(kernel, na, nb, scales), out_shape=pltpu...  62.2 us

profile of v2, /device:TPU:17, one launch (start us, length us, event | category | flops | bytes accessed | tf_op | source)
XLA Modules:
  0.0 63.2 jit_solution(6911631491737297232)
XLA Ops:
  0.0 62.2 %shard_map.37.state_ref = f32[2,32,32,128]{3,2,1,0:T(8,128)S(1)} custom-call(f32[2,32,32,128]{3,2,1,0:T(8,128)} %bitcast.3, f32[32,32,128]{2,1,0:T(8,128)} %bitcast.4, f32[2,128]{1,0:T(2,128)} %angle_hbm.1), custom_call_target="tpu_custom_call" | custom-call | tf_op jit(solution)/shard_map/pallas_call | solution.py:290
  62.3 1.0 %shard_map.38 = f32[2,32,32,128]{3,2,1,0:T(8,128)} custom-call(f32[2,32,32,128]{3,2,1,0:T(8,128)S(1)} %shard_map.37.state_ref), custom_call_target="tpu_custom_call" | custom-call | tf_op jit(solution)/shard_map/pallas_call | solution.py:317

commit v3 on v1

--- a/solution.py
+++ b/solution.py
@@ -91,7 +91,7 @@
 def kernel(
     na, nb, scales, wave_hbm, level_hbm, angle_hbm, out_ref,
     wave, level, angle, rows_table, lanes_table, mixed, send0, got0, send1, got1, levels, cosine, sine,
-    load_sem, own_sem, ssem, rsem, level_sem,
+    load_sem, own_sem, ssem, rsem, level_sem, greet_sem,
 ):
     n = na * nb
     cuts, _, _, step, lanes = send0.shape
@@ -119,13 +119,6 @@
     load_angle.start()
     load_wave.start()
 
-    barrier = pltpu.get_barrier_semaphore()
-    for to_a, to_b, _ in peers[::-1]:
-        pl.semaphore_signal(barrier, inc=1, device_id=(to_a, to_b), device_id_type=MESH)
-
-    load_level.wait()
-    pl.semaphore_wait(barrier, n - 1)
-
     def exchange(source, target, own, sent, got):
         pltpu.make_async_copy(source.at[me], target.at[me], own).start()
         for to_a, to_b, to in peers:
@@ -143,7 +136,78 @@
         rest = source.at[pl.ds(0, n - 1)]
         pltpu.make_async_copy(rest, rest, sent).wait()
 
-    exchange(level, levels, level_sem.at[0], level_sem.at[1], level_sem.at[2])
+    inner = min(na, 4)
+    depth = na // inner
+    z, core = qa // inner, lax.rem(qa, 2)
+    steps = [("qa", 2)] * (inner == 4) + [("qb", 1 << k) for k in range(nb.bit_length() - 1)]
+    sides = []
+    for mask in range(1 << len(steps)):
+        side_a, side_b, later = lax.rem(qa, inner), qb, jnp.int32(0)
+        for k, (axis, bit) in enumerate(steps):
+            if mask >> k & 1:
+                there = lax.rem((qa if axis == "qa" else qb) // bit, 2)
+                later += 1 - there
+                side_a += (bit - 2 * bit * there) * (axis == "qa")
+                side_b += (bit - 2 * bit * there) * (axis == "qb")
+        sides.append((mask.bit_count(), later, side_a, side_b))
+
+    def below(size, later):
+        return later == 0
+
+    def above(size, later):
+        return later == size
+
+    def tell(sem_of, low, high, chosen, both):
+        for mask, (size, later, a, b) in enumerate(sides):
+            for other in range(1 + both):
+
+                @pl.when(chosen(size, later))
+                def _():
+                    skip = not mask and not other
+                    bounds = (low + (skip and chosen is above), high - (skip and chosen is below))
+
+                    def one(to_z, _):
+                        to_a = to_z * inner + a + other * (1 - 2 * core)
+                        pl.semaphore_signal(sem_of(size, to_z), inc=1, device_id=(to_a, b), device_id_type=MESH)
+
+                    lax.fori_loop(*bounds, one, None)
+
+    def send_levels(found):
+        for mask, (_, later, a, b) in enumerate(sides):
+            for other in range(2):
+                ahead = z + found - later
+                own_chip = 1 if not mask and not other else 0
+                low = jnp.where(later < found, ahead, 0)
+                high = jnp.where(later < found, jnp.minimum(ahead + 1, depth), jnp.where(later == found, z + 1 - own_chip, 0))
+
+                def one(to_z, _):
+                    to_a = to_z * inner + a + other * (1 - 2 * core)
+                    pltpu.make_async_remote_copy(
+                        src_ref=level.at[to_a * nb + b], dst_ref=levels.at[me],
+                        send_sem=level_sem.at[1], recv_sem=level_sem.at[2],
+                        device_id=(to_a, b), device_id_type=MESH,
+                    ).start()
+
+                lax.fori_loop(low, high, one, None)
+
+    barrier = pltpu.get_barrier_semaphore()
+    tell(lambda size, to_z: barrier, z, depth, above, True)
+    nearer = sum(jnp.where(below(size, later), 1, 0) for size, later, _, _ in sides)
+    pl.semaphore_wait(barrier, 2 * (z + 1) * nearer - 1)
+    tell(lambda size, to_z: greet_sem.at[size + z - to_z - 1], 0, z + 1, below, False)
+    load_level.wait()
+    send_levels(0)
+    pltpu.make_async_copy(level.at[me], levels.at[me], level_sem.at[0]).start()
+    for found in range(1, len(steps) + depth):
+        fresh = sum(
+            jnp.where(above(size, later) & (found >= size) & (z + found - size < depth), 1, 0) for size, later, _, _ in sides
+        )
+
+        @pl.when(fresh > 0)
+        def _():
+            pl.semaphore_wait(greet_sem.at[found - 1], fresh)
+            send_levels(found)
+
     rows_table[...] = sign_table(n * step)
     lanes_table[...] = sign_table(lanes)
     load_angle.wait()
@@ -264,6 +328,7 @@
             pltpu.SemaphoreType.DMA((2, cuts)),
             pltpu.SemaphoreType.DMA((2, cuts)),
             pltpu.SemaphoreType.DMA((3,)),
+            pltpu.SemaphoreType.REGULAR((nb.bit_length() + na,)),
         ],
         compiler_params=pltpu.CompilerParams(
             collective_id=0, has_side_effects=True, vmem_limit_bytes=SPACE

time: 64.1 us -> 63.2 us (0.986)
  Pallas kernels: 63.8 us -> 63.1 us
    pallas_call x1, Pallas kernels: 62.8 us -> 62.1 us  [body(): pl.pallas_call(functools.partial(kernel, na, nb, scales), out_shape=pltpu...]
where the time goes in v3:
time: 63.2 us; the launch traced here: 63.1 us
  Pallas kernels  63.1 us (100%)
    pallas_call x1, Pallas kernels, body(): pl.pallas_call(functools.partial(kernel, na, nb, scales), out_shape=pltpu...  62.1 us

profile of v3, /device:TPU:17, one launch (start us, length us, event | category | flops | bytes accessed | tf_op | source)
XLA Modules:
  0.0 63.1 jit_solution(1923330977212085716)
XLA Ops:
  0.0 62.1 %shard_map.37.state_ref = f32[2,32,32,128]{3,2,1,0:T(8,128)S(1)} custom-call(f32[2,32,32,128]{3,2,1,0:T(8,128)} %bitcast.3, f32[32,32,128]{2,1,0:T(8,128)} %bitcast.4, f32[2,128]{1,0:T(2,128)} %angle_hbm.1), custom_call_target="tpu_custom_call" | custom-call | tf_op jit(solution)/shard_map/pallas_call | solution.py:313
  62.1 1.0 %shard_map.38 = f32[2,32,32,128]{3,2,1,0:T(8,128)} custom-call(f32[2,32,32,128]{3,2,1,0:T(8,128)S(1)} %shard_map.37.state_ref), custom_call_target="tpu_custom_call" | custom-call | tf_op jit(solution)/shard_map/pallas_call | solution.py:340

commit v4 on v3

--- a/solution.py
+++ b/solution.py
@@ -109,7 +109,7 @@
         return found
 
     to_as, to_bs = flips(qa, na), flips(qb, nb)
-    order = [(ka, kb) for ka in far_first(na) for kb in range(nb) if ka or kb]
+    order = far_first(na, nb)
     peers = [(to_as[ka], to_bs[kb], to_as[ka] * nb + to_bs[kb]) for ka, kb in order]
 
     load_wave = pltpu.make_async_copy(wave_hbm, wave, load_sem.at[0])
@@ -286,10 +286,15 @@
     copy.wait()
 
 
-def far_first(count):
-    quarter = count // 4
-    low = [*range(0, quarter, 2), *range(1, quarter, 2)]
-    return [high * quarter + k for high in (2, 3, 1, 0) for k in low] if quarter else range(count - 1, -1, -1)
+def far_first(na, nb):
+    inner = min(na, 4)
+
+    def rank(offset):
+        ka, kb = offset
+        high, aside, core = ka // inner, ka % inner // 2 + kb.bit_count(), ka % 2
+        return high >= na // inner // 2, high, -aside, core
+
+    return sorted([(ka, kb) for ka in range(na) for kb in range(nb) if ka or kb], key=rank)
 
 
 STEP = 16

time: 63.2 us -> 61.9 us (0.979)
  Pallas kernels: 63.1 us -> 61.8 us
    pallas_call x1, Pallas kernels: 62.1 us -> 60.8 us  [body(): pl.pallas_call(functools.partial(kernel, na, nb, scales), out_shape=pltpu...]
where the time goes in v4:
time: 61.9 us; the launch traced here: 61.8 us
  Pallas kernels  61.8 us (100%)
    pallas_call x1, Pallas kernels, body(): pl.pallas_call(functools.partial(kernel, na, nb, scales), out_shape=pltpu...  60.8 us

profile of v4, /device:TPU:17, one launch (start us, length us, event | category | flops | bytes accessed | tf_op | source)
XLA Modules:
  0.0 61.8 jit_solution(12715897921403855988)
XLA Ops:
  0.0 60.8 %shard_map.37.state_ref = f32[2,32,32,128]{3,2,1,0:T(8,128)S(1)} custom-call(f32[2,32,32,128]{3,2,1,0:T(8,128)} %bitcast.3, f32[32,32,128]{2,1,0:T(8,128)} %bitcast.4, f32[2,128]{1,0:T(2,128)} %angle_hbm.1), custom_call_target="tpu_custom_call" | custom-call | tf_op jit(solution)/shard_map/pallas_call | solution.py:318
  60.8 1.0 %shard_map.38 = f32[2,32,32,128]{3,2,1,0:T(8,128)} custom-call(f32[2,32,32,128]{3,2,1,0:T(8,128)S(1)} %shard_map.37.state_ref), custom_call_target="tpu_custom_call" | custom-call | tf_op jit(solution)/shard_map/pallas_call | solution.py:345

commit v5 on v4

--- a/solution.py
+++ b/solution.py
@@ -89,9 +89,9 @@
 
 
 def kernel(
-    na, nb, scales, wave_hbm, level_hbm, angle_hbm, out_ref,
-    wave, level, angle, rows_table, lanes_table, mixed, send0, got0, send1, got1, levels, cosine, sine,
-    load_sem, own_sem, ssem, rsem, level_sem, greet_sem,
+    na, nb, scales, wave_hbm, level_hbm, angle_hbm, got1, mixed_ref,
+    wave, level, angle, rows_table, lanes_table, mixed, send0, got0, send1, levels, cosine, sine,
+    load_sem, ssem, rsem, level_sem, greet_sem,
 ):
     n = na * nb
     cuts, _, _, step, lanes = send0.shape
@@ -117,20 +117,17 @@
     load_angle = pltpu.make_async_copy(angle_hbm, angle, load_sem.at[2])
     load_level.start()
     load_angle.start()
-    load_wave.start()
-
-    def exchange(source, target, own, sent, got):
-        pltpu.make_async_copy(source.at[me], target.at[me], own).start()
+
+    def exchange(source, target, sent, got):
+        pltpu.make_async_copy(source.at[me], target.at[me], got).start()
         for to_a, to_b, to in peers:
             pltpu.make_async_remote_copy(
                 src_ref=source.at[to], dst_ref=target.at[me], send_sem=sent, recv_sem=got,
                 device_id=(to_a, to_b), device_id_type=MESH,
             ).start()
 
-    def received(source, target, own, got):
-        pltpu.make_async_copy(source.at[me], target.at[me], own).wait()
-        rest = target.at[pl.ds(0, n - 1)]
-        pltpu.make_async_copy(rest, rest, got).wait()
+    def received(target, got):
+        pltpu.make_async_copy(target, target, got).wait()
 
     def left(source, sent):
         rest = source.at[pl.ds(0, n - 1)]
@@ -164,9 +161,10 @@
                 @pl.when(chosen(size, later))
                 def _():
                     skip = not mask and not other
-                    bounds = (low + (skip and chosen is above), high - (skip and chosen is below))
-
-                    def one(to_z, _):
+                    bounds = (low + (not mask and not other), high)
+
+                    def one(at, _):
+                        to_z = at if chosen is above else z - at
                         to_a = to_z * inner + a + other * (1 - 2 * core)
                         pl.semaphore_signal(sem_of(size, to_z), inc=1, device_id=(to_a, b), device_id_type=MESH)
 
@@ -184,7 +182,7 @@
                     to_a = to_z * inner + a + other * (1 - 2 * core)
                     pltpu.make_async_remote_copy(
                         src_ref=level.at[to_a * nb + b], dst_ref=levels.at[me],
-                        send_sem=level_sem.at[1], recv_sem=level_sem.at[2],
+                        send_sem=level_sem.at[0], recv_sem=level_sem.at[1],
                         device_id=(to_a, b), device_id_type=MESH,
                     ).start()
 
@@ -196,8 +194,9 @@
     pl.semaphore_wait(barrier, 2 * (z + 1) * nearer - 1)
     tell(lambda size, to_z: greet_sem.at[size + z - to_z - 1], 0, z + 1, below, False)
     load_level.wait()
+    load_wave.start()
     send_levels(0)
-    pltpu.make_async_copy(level.at[me], levels.at[me], level_sem.at[0]).start()
+    pltpu.make_async_copy(level.at[me], levels.at[me], level_sem.at[1]).start()
     for found in range(1, len(steps) + depth):
         fresh = sum(
             jnp.where(above(size, later) & (found >= size) & (z + found - size < depth), 1, 0) for size, later, _, _ in sides
@@ -234,9 +233,9 @@
 
     @pl.loop(0, cuts)
     def _(cut):
-        exchange(send0.at[cut], got0.at[cut], own_sem.at[0, cut], ssem.at[0, cut], rsem.at[0, cut])
-
-    received(level, levels, level_sem.at[0], level_sem.at[2])
+        exchange(send0.at[cut], got0.at[cut], ssem.at[0, cut], rsem.at[0, cut])
+
+    received(levels, level_sem.at[1])
     second = angle[1:2, :]
 
     @pl.loop(0, n)
@@ -247,7 +246,7 @@
 
     @pl.loop(0, cuts)
     def _(cut):
-        received(send0.at[cut], got0.at[cut], own_sem.at[0, cut], rsem.at[0, cut])
+        received(got0.at[cut], rsem.at[0, cut])
         held = pl.ds(pl.multiple_of(cut * step, step), step)
         x, y = mix_lead(got0[cut, :, 0]), mix_lead(got0[cut, :, 1])
         c, s = cosine[:, held, :], sine[:, held, :]
@@ -255,24 +254,18 @@
         done = mix_rows_lanes(rows_table[...], lanes_table[...], x, y)
         for part in range(2):
             send1[cut, :, part] = done[part].reshape(n, step, lanes)
-        exchange(send1.at[cut], got1.at[cut], own_sem.at[1, cut], ssem.at[1, cut], rsem.at[1, cut])
+        exchange(send1.at[cut], got1.at[cut], ssem.at[1, cut], rsem.at[1, cut])
 
     few = min(8, step)
     for cut in range(cuts):
-        received(send1.at[cut], got1.at[cut], own_sem.at[1, cut], rsem.at[1, cut])
-        last = cut == cuts - 1
-
+        received(got1.at[cut], rsem.at[1, cut])
+        if cut == cuts - 1:
+            continue
         for part in range(2):
             for row in range(0, step, few):
-                done = mix_lead(got1[cut, :, part, row : row + few])
-                if not last:
-                    mixed[cut, part, :, row : row + few] = done
-                    continue
-                parts = [mixed[k, part, :, row : row + few] for k in range(cut)] + [done]
-                for k, value in enumerate(mix_list(parts)):
-                    out_ref[part, :, k * step + row : k * step + row + few, :] = value
-
-    left(level, level_sem.at[1])
+                mixed_ref[cut, part, :, row : row + few] = mix_lead(got1[cut, :, part, row : row + few])
+
+    left(level, level_sem.at[0])
 
     @pl.loop(0, cuts)
     def _(cut):
@@ -280,10 +273,19 @@
         left(send1.at[cut], ssem.at[1, cut])
 
 
-def put_out(state_ref, out_hbm, sem):
-    copy = pltpu.make_async_copy(state_ref, out_hbm, sem)
-    copy.start()
-    copy.wait()
+def put_out(got_ref, mixed_ref, out_hbm, out, sem):
+    cuts, _, _, step, _ = mixed_ref.shape
+    few = min(8, step)
+    for row in range(0, step, few):
+        for part in range(2):
+            done = mix_lead(got_ref[cuts - 1, :, part, row : row + few])
+            parts = [mixed_ref[k, part, :, row : row + few] for k in range(cuts - 1)] + [done]
+            for k, value in enumerate(mix_list(parts)):
+                out[part, :, k * step + row : k * step + row + few, :] = value
+        for k in range(cuts):
+            rows = pl.ds(k * step + row, few)
+            pltpu.make_async_copy(out.at[:, :, rows], out_hbm.at[:, :, rows], sem).start()
+    pltpu.make_async_copy(out, out_hbm, sem).wait()
 
 
 def far_first(na, nb):
@@ -317,9 +319,9 @@
     table = pltpu.VMEM((n, piece, lanes), f32)
     result = pl.pallas_call(
         functools.partial(kernel, na, nb, scales),
-        out_shape=pltpu.VMEM(flat, f32),
+        out_shape=(pltpu.VMEM(state.shape, f32), pltpu.VMEM((cuts, 2, n, step, lanes), f32)),
         in_specs=[hbm, hbm, hbm],
-        out_specs=pl.BlockSpec(memory_space=pltpu.VMEM),
+        out_specs=(pl.BlockSpec(memory_space=pltpu.VMEM),) * 2,
         scratch_shapes=[
             pltpu.VMEM(flat, f32),
             table,
@@ -327,13 +329,12 @@
             pltpu.VMEM((n * step, n * step), jnp.bfloat16),
             pltpu.VMEM((lanes, lanes), jnp.bfloat16),
             pltpu.VMEM((cuts, 2, n, step, lanes), f32),
-            state, state, state, state, table, table, table,
+            state, state, state, table, table, table,
             pltpu.SemaphoreType.DMA((3,)),
             pltpu.SemaphoreType.DMA((2, cuts)),
             pltpu.SemaphoreType.DMA((2, cuts)),
-            pltpu.SemaphoreType.DMA((2, cuts)),
-            pltpu.SemaphoreType.DMA((3,)),
-            pltpu.SemaphoreType.REGULAR((nb.bit_length() + na,)),
+            pltpu.SemaphoreType.DMA((2,)),
+            pltpu.SemaphoreType.REGULAR((nb.bit_length() + max(na // 4, 1),)),
         ],
         compiler_params=pltpu.CompilerParams(
             collective_id=0, has_side_effects=True, vmem_limit_bytes=SPACE
@@ -345,11 +346,11 @@
     result = pl.pallas_call(
         put_out,
         out_shape=jax.ShapeDtypeStruct(flat, f32),
-        in_specs=[pl.BlockSpec(memory_space=pltpu.VMEM)],
+        in_specs=[pl.BlockSpec(memory_space=pltpu.VMEM)] * 2,
         out_specs=hbm,
-        scratch_shapes=[pltpu.SemaphoreType.DMA],
-        compiler_params=pltpu.CompilerParams(vmem_limit_bytes=4 * 2**20),
-    )(result)
+        scratch_shapes=[pltpu.VMEM(flat, f32), pltpu.SemaphoreType.DMA],
+        compiler_params=pltpu.CompilerParams(vmem_limit_bytes=8 * 2**20),
+    )(*result)
     return result.reshape(wave_parts.shape)
 
 

time: 61.9 us -> 61.7 us (level)
  no operation moved by 1% of the time
where the time goes in v5:
time: 61.7 us; the launch traced here: 61.5 us
  Pallas kernels  61.5 us (100%)
    pallas_call x1, Pallas kernels, body(): pl.pallas_call(functools.partial(kernel, na, nb, scales), out_shape=(pltp...  60.4 us

profile of v5, /device:TPU:17, one launch (start us, length us, event | category | flops | bytes accessed | tf_op | source)
XLA Modules:
  0.0 61.5 jit_solution(10089464573596890375)
XLA Ops:
  0.0 60.4 %shard_map.37 = (f32[2,32,2,16,128]{4,3,2,1,0:T(8,128)S(1)}, f32[2,2,32,16,128]{4,3,2,1,0:T(8,128)S(1)}) custom-call(f32[2,32,32,128]{3,2,1,0:T(8,128)} %bitcast.3, f32[32,32,128]{2,1,0:T(8,128)} %bitcast.4, f32[2,128]{1,0:T(2,128)} %angle_hbm.1), custom_call_target="tpu_custom_call" | custom-call | tf_op jit(solution)/shard_map/pallas_call | solution.py:320
  60.4 1.1 %shard_map.38 = f32[2,32,32,128]{3,2,1,0:T(8,128)} custom-call(f32[2,32,2,16,128]{4,3,2,1,0:T(8,128)S(1)} %get-tuple-element.7.got_ref, f32[2,2,32,16,128]{4,3,2,1,0:T(8,128)S(1)} %get-tuple-element.8.mixed_ref), custom_call_target="tpu_custom_call" | custom-call | tf_op jit(solution)/shard_map/pallas_call | solution.py:346

commit v6 on v5

--- a/solution.py
+++ b/solution.py
@@ -109,8 +109,17 @@
         return found
 
     to_as, to_bs = flips(qa, na), flips(qb, nb)
-    order = far_first(na, nb)
-    peers = [(to_as[ka], to_bs[kb], to_as[ka] * nb + to_bs[kb]) for ka, kb in order]
+    aside = lax.rem(qa // 2, 2) == 1
+
+    def place(ka, kb):
+        to_a, to_b = to_as[ka], to_bs[kb]
+        if min(na, 4) == 4 and kb < 2 and ka // 2 % 2 != kb:
+            to_a, to_b = jnp.where(aside, to_a, to_as[ka ^ 2]), jnp.where(aside, to_b, to_bs[kb ^ 1])
+        if ka > 1 or kb:
+            to_a += 1 - ka % 2 - lax.rem(to_a, 2)
+        return to_a, to_b, to_a * nb + to_b
+
+    peers = [place(ka, kb) for ka, kb in far_first(na, nb)]
 
     load_wave = pltpu.make_async_copy(wave_hbm, wave, load_sem.at[0])
     load_level = pltpu.make_async_copy(level_hbm, level, load_sem.at[1])
@@ -281,10 +290,9 @@
             done = mix_lead(got_ref[cuts - 1, :, part, row : row + few])
             parts = [mixed_ref[k, part, :, row : row + few] for k in range(cuts - 1)] + [done]
             for k, value in enumerate(mix_list(parts)):
-                out[part, :, k * step + row : k * step + row + few, :] = value
-        for k in range(cuts):
-            rows = pl.ds(k * step + row, few)
-            pltpu.make_async_copy(out.at[:, :, rows], out_hbm.at[:, :, rows], sem).start()
+                rows = pl.ds(k * step + row, few)
+                out[part, :, rows, :] = value
+                pltpu.make_async_copy(out.at[part, :, rows], out_hbm.at[part, :, rows], sem).start()
     pltpu.make_async_copy(out, out_hbm, sem).wait()
 
 
@@ -294,7 +302,7 @@
     def rank(offset):
         ka, kb = offset
         high, aside, core = ka // inner, ka % inner // 2 + kb.bit_count(), ka % 2
-        return high >= na // inner // 2, high, -aside, core
+        return high >= na // inner // 2, high, -aside, ka % inner < 2, core
 
     return sorted([(ka, kb) for ka in range(na) for kb in range(nb) if ka or kb], key=rank)
 

time: 61.7 us -> 61.5 us (level)
  no operation moved by 1% of the time
where the time goes in v6:
time: 61.5 us; the launch traced here: 61.2 us
  Pallas kernels  61.2 us (100%)
    pallas_call x1, Pallas kernels, body(): pl.pallas_call(functools.partial(kernel, na, nb, scales), out_shape=(pltp...  60.2 us

profile of v6, /device:TPU:17, one launch (start us, length us, event | category | flops | bytes accessed | tf_op | source)
XLA Modules:
  0.0 61.2 jit_solution(176510393771123052)
XLA Ops:
  0.0 60.2 %shard_map.37 = (f32[2,32,2,16,128]{4,3,2,1,0:T(8,128)S(1)}, f32[2,2,32,16,128]{4,3,2,1,0:T(8,128)S(1)}) custom-call(f32[2,32,32,128]{3,2,1,0:T(8,128)} %bitcast.3, f32[32,32,128]{2,1,0:T(8,128)} %bitcast.4, f32[2,128]{1,0:T(2,128)} %angle_hbm.1), custom_call_target="tpu_custom_call" | custom-call | tf_op jit(solution)/shard_map/pallas_call | solution.py:328
  60.2 1.0 %shard_map.38 = f32[2,32,32,128]{3,2,1,0:T(8,128)} custom-call(f32[2,32,2,16,128]{4,3,2,1,0:T(8,128)S(1)} %get-tuple-element.7.got_ref, f32[2,2,32,16,128]{4,3,2,1,0:T(8,128)S(1)} %get-tuple-element.8.mixed_ref), custom_call_target="tpu_custom_call" | custom-call | tf_op jit(solution)/shard_map/pallas_call | solution.py:354

commit v7 on v6

--- a/solution.py
+++ b/solution.py
@@ -89,7 +89,7 @@
 
 
 def kernel(
-    na, nb, scales, wave_hbm, level_hbm, angle_hbm, got1, mixed_ref,
+    na, nb, scales, wave_hbm, level_hbm, angle_hbm, got1,
     wave, level, angle, rows_table, lanes_table, mixed, send0, got0, send1, levels, cosine, sine,
     load_sem, ssem, rsem, level_sem, greet_sem,
 ):
@@ -127,9 +127,10 @@
     load_level.start()
     load_angle.start()
 
-    def exchange(source, target, sent, got):
-        pltpu.make_async_copy(source.at[me], target.at[me], got).start()
-        for to_a, to_b, to in peers:
+    def exchange(source, target, sent, got, chosen=slice(None)):
+        if chosen.stop is None:
+            pltpu.make_async_copy(source.at[me], target.at[me], got).start()
+        for to_a, to_b, to in peers[chosen]:
             pltpu.make_async_remote_copy(
                 src_ref=source.at[to], dst_ref=target.at[me], send_sem=sent, recv_sem=got,
                 device_id=(to_a, to_b), device_id_type=MESH,
@@ -263,16 +264,16 @@
         done = mix_rows_lanes(rows_table[...], lanes_table[...], x, y)
         for part in range(2):
             send1[cut, :, part] = done[part].reshape(n, step, lanes)
-        exchange(send1.at[cut], got1.at[cut], ssem.at[1, cut], rsem.at[1, cut])
-
-    few = min(8, step)
-    for cut in range(cuts):
+        pltpu.make_async_copy(send1.at[cut, me], got1.at[cut, me], rsem.at[1, cut]).start()
+        exchange(send1.at[cut], got1.at[cut], ssem.at[1, cut], rsem.at[1, cut], slice(0, n - 1 - LATE))
+
+    @pl.loop(0, cuts)
+    def _(cut):
+        exchange(send1.at[cut], got1.at[cut], ssem.at[1, cut], rsem.at[1, cut], slice(n - 1 - LATE, n))
+
+    @pl.loop(0, cuts)
+    def _(cut):
         received(got1.at[cut], rsem.at[1, cut])
-        if cut == cuts - 1:
-            continue
-        for part in range(2):
-            for row in range(0, step, few):
-                mixed_ref[cut, part, :, row : row + few] = mix_lead(got1[cut, :, part, row : row + few])
 
     left(level, level_sem.at[0])
 
@@ -282,13 +283,12 @@
         left(send1.at[cut], ssem.at[1, cut])
 
 
-def put_out(got_ref, mixed_ref, out_hbm, out, sem):
-    cuts, _, _, step, _ = mixed_ref.shape
+def put_out(got_ref, out_hbm, out, sem):
+    cuts, _, _, step, _ = got_ref.shape
     few = min(8, step)
     for row in range(0, step, few):
         for part in range(2):
-            done = mix_lead(got_ref[cuts - 1, :, part, row : row + few])
-            parts = [mixed_ref[k, part, :, row : row + few] for k in range(cuts - 1)] + [done]
+            parts = [mix_lead(got_ref[k, :, part, row : row + few]) for k in range(cuts)]
             for k, value in enumerate(mix_list(parts)):
                 rows = pl.ds(k * step + row, few)
                 out[part, :, rows, :] = value
@@ -308,6 +308,7 @@
 
 
 STEP = 16
+LATE = 2
 SPACE = 40 * 2**20
 
 
@@ -327,9 +328,9 @@
     table = pltpu.VMEM((n, piece, lanes), f32)
     result = pl.pallas_call(
         functools.partial(kernel, na, nb, scales),
-        out_shape=(pltpu.VMEM(state.shape, f32), pltpu.VMEM((cuts, 2, n, step, lanes), f32)),
+        out_shape=pltpu.VMEM(state.shape, f32),
         in_specs=[hbm, hbm, hbm],
-        out_specs=(pl.BlockSpec(memory_space=pltpu.VMEM),) * 2,
+        out_specs=pl.BlockSpec(memory_space=pltpu.VMEM),
         scratch_shapes=[
             pltpu.VMEM(flat, f32),
             table,
@@ -354,11 +355,11 @@
     result = pl.pallas_call(
         put_out,
         out_shape=jax.ShapeDtypeStruct(flat, f32),
-        in_specs=[pl.BlockSpec(memory_space=pltpu.VMEM)] * 2,
+        in_specs=[pl.BlockSpec(memory_space=pltpu.VMEM)],
         out_specs=hbm,
         scratch_shapes=[pltpu.VMEM(flat, f32), pltpu.SemaphoreType.DMA],
         compiler_params=pltpu.CompilerParams(vmem_limit_bytes=8 * 2**20),
-    )(*result)
+    )(result)
     return result.reshape(wave_parts.shape)
 
 

time: 61.5 us -> 61.4 us (level)
  no operation moved by 1% of the time
where the time goes in v7:
time: 61.4 us; the launch traced here: 61.3 us
  Pallas kernels  61.3 us (100%)
    pallas_call x1, Pallas kernels, body(): pl.pallas_call(functools.partial(kernel, na, nb, scales), out_shape=pltpu...  60.2 us

profile of v7, /device:TPU:17, one launch (start us, length us, event | category | flops | bytes accessed | tf_op | source)
XLA Modules:
  0.0 61.3 jit_solution(214338857204256594)
XLA Ops:
  0.0 60.2 %shard_map.37.got_ref = f32[2,32,2,16,128]{4,3,2,1,0:T(8,128)S(1)} custom-call(f32[2,32,32,128]{3,2,1,0:T(8,128)} %bitcast.3, f32[32,32,128]{2,1,0:T(8,128)} %bitcast.4, f32[2,128]{1,0:T(2,128)} %angle_hbm.1), custom_call_target="tpu_custom_call" | custom-call | tf_op jit(solution)/shard_map/pallas_call | solution.py:329
  60.2 1.1 %shard_map.38 = f32[2,32,32,128]{3,2,1,0:T(8,128)} custom-call(f32[2,32,2,16,128]{4,3,2,1,0:T(8,128)S(1)} %shard_map.37.got_ref), custom_call_target="tpu_custom_call" | custom-call | tf_op jit(solution)/shard_map/pallas_call | solution.py:355

commit v8 on v7

--- a/solution.py
+++ b/solution.py
@@ -90,11 +90,12 @@
 
 def kernel(
     na, nb, scales, wave_hbm, level_hbm, angle_hbm, got1,
-    wave, level, angle, rows_table, lanes_table, mixed, send0, got0, send1, levels, cosine, sine,
+    wave, level, angle, rows_table, lanes_table, mixed, sends, got0, levels, cosine, sine,
     load_sem, ssem, rsem, level_sem, greet_sem,
 ):
     n = na * nb
-    cuts, _, _, step, lanes = send0.shape
+    _, cuts, _, _, step, lanes = sends.shape
+    send0, send1 = sends.at[0], sends.at[1]
     qa, qb = lax.axis_index("qa"), lax.axis_index("qb")
     me = qa * nb + qb
     group = 4
@@ -243,7 +244,7 @@
 
     @pl.loop(0, cuts)
     def _(cut):
-        exchange(send0.at[cut], got0.at[cut], ssem.at[0, cut], rsem.at[0, cut])
+        exchange(send0.at[cut], got0.at[cut], ssem, rsem.at[0, cut])
 
     received(levels, level_sem.at[1])
     second = angle[1:2, :]
@@ -265,22 +266,19 @@
         for part in range(2):
             send1[cut, :, part] = done[part].reshape(n, step, lanes)
         pltpu.make_async_copy(send1.at[cut, me], got1.at[cut, me], rsem.at[1, cut]).start()
-        exchange(send1.at[cut], got1.at[cut], ssem.at[1, cut], rsem.at[1, cut], slice(0, n - 1 - LATE))
-
-    @pl.loop(0, cuts)
-    def _(cut):
-        exchange(send1.at[cut], got1.at[cut], ssem.at[1, cut], rsem.at[1, cut], slice(n - 1 - LATE, n))
+        exchange(send1.at[cut], got1.at[cut], ssem, rsem.at[1, cut], slice(0, n - 1 - LATE))
+
+    @pl.loop(0, cuts)
+    def _(cut):
+        exchange(send1.at[cut], got1.at[cut], ssem, rsem.at[1, cut], slice(n - 1 - LATE, n))
 
     @pl.loop(0, cuts)
     def _(cut):
         received(got1.at[cut], rsem.at[1, cut])
 
     left(level, level_sem.at[0])
-
-    @pl.loop(0, cuts)
-    def _(cut):
-        left(send0.at[cut], ssem.at[0, cut])
-        left(send1.at[cut], ssem.at[1, cut])
+    rest = sends.at[:, :, pl.ds(0, n - 1)]
+    pltpu.make_async_copy(rest, rest, ssem).wait()
 
 
 def put_out(got_ref, out_hbm, out, sem):
@@ -302,7 +300,9 @@
     def rank(offset):
         ka, kb = offset
         high, aside, core = ka // inner, ka % inner // 2 + kb.bit_count(), ka % 2
-        return high >= na // inner // 2, high, -aside, ka % inner < 2, core
+        crossing, last = high >= na // inner // 2, high == na // inner - 1
+        weight = 20 * crossing + 5 * last - aside + (ka % inner < 2) + (high == 1) + 4 * (last and not aside)
+        return weight, high, aside
 
     return sorted([(ka, kb) for ka in range(na) for kb in range(nb) if ka or kb], key=rank)
 
@@ -338,9 +338,9 @@
             pltpu.VMEM((n * step, n * step), jnp.bfloat16),
             pltpu.VMEM((lanes, lanes), jnp.bfloat16),
             pltpu.VMEM((cuts, 2, n, step, lanes), f32),
-            state, state, state, table, table, table,
+            pltpu.VMEM((2, *state.shape), f32), state, table, table, table,
             pltpu.SemaphoreType.DMA((3,)),
-            pltpu.SemaphoreType.DMA((2, cuts)),
+            pltpu.SemaphoreType.DMA,
             pltpu.SemaphoreType.DMA((2, cuts)),
             pltpu.SemaphoreType.DMA((2,)),
             pltpu.SemaphoreType.REGULAR((nb.bit_length() + max(na // 4, 1),)),

time: 61.4 us -> 61.4 us (level)
  no operation moved by 1% of the time
where the time goes in v8:
time: 61.4 us; the launch traced here: 61.2 us
  Pallas kernels  61.2 us (100%)
    pallas_call x1, Pallas kernels, body(): pl.pallas_call(functools.partial(kernel, na, nb, scales), out_shape=pltpu...  60.2 us

profile of v8, /device:TPU:17, one launch (start us, length us, event | category | flops | bytes accessed | tf_op | source)
XLA Modules:
  0.0 61.2 jit_solution(2351843859885996736)
XLA Ops:
  0.0 60.2 %shard_map.37.got_ref = f32[2,32,2,16,128]{4,3,2,1,0:T(8,128)S(1)} custom-call(f32[2,32,32,128]{3,2,1,0:T(8,128)} %bitcast.3, f32[32,32,128]{2,1,0:T(8,128)} %bitcast.4, f32[2,128]{1,0:T(2,128)} %angle_hbm.1), custom_call_target="tpu_custom_call" | custom-call | tf_op jit(solution)/shard_map/pallas_call | solution.py:329
  60.2 1.1 %shard_map.38 = f32[2,32,32,128]{3,2,1,0:T(8,128)} custom-call(f32[2,32,2,16,128]{4,3,2,1,0:T(8,128)S(1)} %shard_map.37.got_ref), custom_call_target="tpu_custom_call" | custom-call | tf_op jit(solution)/shard_map/pallas_call | solution.py:355

commit v9 on v8

--- a/solution.py
+++ b/solution.py
@@ -284,8 +284,8 @@
 def put_out(got_ref, out_hbm, out, sem):
     cuts, _, _, step, _ = got_ref.shape
     few = min(8, step)
-    for row in range(0, step, few):
-        for part in range(2):
+    for part in range(2):
+        for row in range(0, step, few):
             parts = [mix_lead(got_ref[k, :, part, row : row + few]) for k in range(cuts)]
             for k, value in enumerate(mix_list(parts)):
                 rows = pl.ds(k * step + row, few)

time: 61.4 us -> 61.4 us (level)
  no operation moved by 1% of the time
where the time goes in v9:
time: 61.4 us; the launch traced here: 61.2 us
  Pallas kernels  61.2 us (100%)
    pallas_call x1, Pallas kernels, body(): pl.pallas_call(functools.partial(kernel, na, nb, scales), out_shape=pltpu...  60.2 us

profile of v9, /device:TPU:17, one launch (start us, length us, event | category | flops | bytes accessed | tf_op | source)
XLA Modules:
  0.0 61.2 jit_solution(7609458793173691923)
XLA Ops:
  0.0 60.2 %shard_map.37.got_ref = f32[2,32,2,16,128]{4,3,2,1,0:T(8,128)S(1)} custom-call(f32[2,32,32,128]{3,2,1,0:T(8,128)} %bitcast.3, f32[32,32,128]{2,1,0:T(8,128)} %bitcast.4, f32[2,128]{1,0:T(2,128)} %angle_hbm.1), custom_call_target="tpu_custom_call" | custom-call | tf_op jit(solution)/shard_map/pallas_call | solution.py:329
  60.2 1.1 %shard_map.38 = f32[2,32,32,128]{3,2,1,0:T(8,128)} custom-call(f32[2,32,2,16,128]{4,3,2,1,0:T(8,128)S(1)} %shard_map.37.got_ref), custom_call_target="tpu_custom_call" | custom-call | tf_op jit(solution)/shard_map/pallas_call | solution.py:355
